TPU v7x, 128 devices: a whole 4x4x4 slice. The times are simulated.
128 devices in a mesh: band: 64 (over y, z, x_hi, core), grid: 2 (over x_lo).
Axes of the slice: x: 4 (x_hi: 2, x_lo: 2; x = x_hi * 2 + x_lo), y: 4, z: 4, core: 2. Of those that a mesh axis runs over, the one named last changes fastest.
Arguments:
- bands: float32 [128, 72, 5184], P('band', 'grid'), may hold values from -2.4 to 2.4
Outputs:
- exchange_terms: float32 [128, 72, 5184], P('band', 'grid')
All inputs are finite; a program needn't handle non-finite values.
Results may differ from a plain program's by a relative error of at most 0.0001.
Values sent between devices are 32-bit elements; how exact they have to be, the bound alone decides.
A program may use at most 128 MiB of HBM per device.

v0:
```python
import math
import jax
import jax.numpy as jnp
from jax import lax
from jax.sharding import PartitionSpec as P

GRID = 72
STEPS = 3
spacing = 0.5167


def shifted(value, axis, steps):
    count = lax.axis_size(axis)
    pairs = [(source, (source + steps) % count) for source in range(count)]
    return lax.ppermute(value, axis, pairs)


def split_up(array, dim, devices):
    before, after = (array.shape[:dim], array.shape[dim + 1 :])
    return jnp.moveaxis(array.reshape(*before, devices, -1, *after), dim, 0)


def sent_and_summed(array, axis, dim):
    devices = lax.axis_size(axis)
    blocks = lax.all_to_all(split_up(array, dim, devices), axis, 0, 0, tiled=True)
    return jnp.sum(blocks, axis=0)


def tables(count):
    index = jnp.arange(count, dtype=jnp.int32)
    half = count // 2
    freq = jnp.where(index <= half, index, index - half)
    phase = (freq[:, None] * index[None, :] % count).astype(jnp.float32) * (2.0 * math.pi / count)
    table = jnp.where(index[:, None] <= half, jnp.cos(phase), jnp.sin(phase))
    weight = jnp.where((index == 0) | (index == half), 1.0, 2.0).astype(jnp.float32)
    square = freq.astype(jnp.float32) ** 2
    factor = (2.0 * math.pi / (count * spacing)) ** 2
    ksq = factor * (square[:, None, None] + square[None, :, None] + square[None, None, :])
    safe = jnp.where(ksq > 0, ksq, 1.0)
    coulomb = jnp.where(ksq > 0, 4.0 * math.pi / safe, 0.0)
    weights = weight[:, None, None] * weight[None, :, None] * weight[None, None, :]
    kernel = coulomb * weights / float(count**3)
    return (table, kernel.reshape(count, count * count))


def forward_axis(values, table):
    return jnp.einsum("pmc,kc->pkm", values, table, precision=lax.Precision.HIGHEST)


def inverse_axis(values, table):
    return jnp.einsum("pmk,kr->prm", values, table, precision=lax.Precision.HIGHEST)


def coulomb_filter(density, table, kernel):
    count = table.shape[0]
    pairs = density.shape[0]
    work = forward_axis(density.reshape(pairs, count * count, count), table)
    work = forward_axis(work.reshape(pairs, count * count, count), table)
    work = forward_axis(work.reshape(pairs, count * count, count), table)
    work = work * kernel[None]
    work = inverse_axis(work.reshape(pairs, count * count, count), table)
    work = inverse_axis(work.reshape(pairs, count * count, count), table)
    work = inverse_axis(work.reshape(pairs, count * count, count), table)
    return work


def pair_terms(home, visit, table, kernel):
    home_count = home.shape[0]
    visit_count = visit.shape[0]
    count = home.shape[1]
    density = (home[:, None] * visit[None]).reshape(home_count * visit_count, count, home.shape[2])
    potential = coulomb_filter(density, table, kernel).reshape(
        home_count, visit_count, count, home.shape[2]
    )
    home_part = -jnp.sum(potential * visit[None], axis=1)
    partner = -jnp.sum(potential * home[:, None], axis=0)
    return (home_part, partner)


def local(bands):
    table, kernel = tables(GRID)
    whole = lax.all_gather(bands, "grid", axis=1, tiled=True)
    share = whole.shape[0] // lax.axis_size("grid")
    first = lax.axis_index("grid") * share
    visit = lax.dynamic_slice_in_dim(whole, first, share, 0)
    home_total = jnp.zeros_like(whole)
    carried = jnp.zeros_like(visit)
    for step in range(STEPS):
        visit = shifted(visit, "band", 1)
        home_part, partner = pair_terms(whole, visit, table, kernel)
        home_total = home_total + home_part
        carried = carried + partner
        if step + 1 < STEPS:
            carried = shifted(carried, "band", 1)
    returned = shifted(carried, "band", -STEPS)
    own_rows = lax.dynamic_slice_in_dim(home_total, first, share, 0) + returned
    home_total = lax.dynamic_update_slice_in_dim(home_total, own_rows, first, 0)
    return sent_and_summed(home_total, "grid", 1)


def solution(mesh):
    return jax.shard_map(
        local,
        mesh=mesh,
        in_specs=(P("band", "grid", None),),
        out_specs=P("band", "grid", None),
        check_vma=False,
    )
```

profile of v0, /device:TPU:4, one launch (start us, length us, event | category | flops | bytes accessed | tf_op | source)
XLA Modules:
  0.0 540.2 jit_solution(13337431884350394181)
XLA Ops:
  7.3 49.8 %all-gather.2.cloned.1.call-done = f32[2,72,5184]{2,0,1:T(2,128)} async-done(((f32[2,36,5184]{2,0,1:T(2,128)}), f32[2,72,5184]{2,0,1:T(2,128)}) %all-gather.2.cloned.1.call-update) | async-done | bytes 2986000 | tf_op jit(solution)/shard_map/all_gather | solution.py:82
  60.3 20.7 %collective-permute-done = f32[1,72,5184]{2,0,1:T(1,128)S(1)} collective-permute-done((f32[1,72,5184]{2,0,1:T(1,128)S(1)}, f32[1,72,5184]{2,0,1:T(1,128)S(1)}, u32[]{:S(2)}, u32[]{:S(2)}) %collective-permute-start) | collective-permute-done | bytes 1493024 | tf_op jit(solution)/shard_map/ppermute | solution.py:15
  82.3 20.6 %collective-permute-done.1 = f32[1,72,5184]{2,0,1:T(1,128)} collective-permute-done((f32[1,72,5184]{2,0,1:T(1,128)S(1)}, f32[1,72,5184]{2,0,1:T(1,128)}, u32[]{:S(2)}, u32[]{:S(2)}) %collective-permute-start.1) | collective-permute-done | bytes 1493024 | tf_op jit(solution)/shard_map/ppermute | solution.py:15
  113.3 10.6 %collective-permute-done.2 = f32[1,72,5184]{2,0,1:T(1,128)} collective-permute-done((f32[1,72,5184]{2,0,1:T(1,128)}, f32[1,72,5184]{2,0,1:T(1,128)}, u32[]{:S(2)}, u32[]{:S(2)}) %collective-permute-start.2) | collective-permute-done | bytes 1493024 | tf_op jit(solution)/shard_map/ppermute | solution.py:15
  135.5 9.4 %convolution_bitcast_fusion.14 = f32[2,72,5184]{2,1,0:T(8,128)} fusion(f32[2,5184,72]{2,1,0:T(8,128)} %reshape_reshape.9, s32[72]{0:T(128)S(1)} %add_select_fusion.1, pred[72]{0:T(512)(128)(4,1)S(1)} %iota_compare_fusion), kind=kOutput, calls=%fused_computation.20 | convolution fusion | flops 645024384 | bytes 5972328 | tf_op jit(solution)/shard_map/pmc,kc->pkm/dot_general | solution.py:47
  150.8 9.4 %convolution_bitcast_fusion.13 = f32[2,72,5184]{2,1,0:T(8,128)} fusion(f32[2,5184,72]{2,1,0:T(8,128)} %reshape.283, s32[72]{0:T(128)S(1)} %add_select_fusion.1, pred[72]{0:T(512)(128)(4,1)S(1)} %iota_compare_fusion), kind=kOutput, calls=%fused_computation.19 | convolution fusion | flops 645024384 | bytes 5972328 | tf_op jit(solution)/shard_map/pmc,kc->pkm/dot_general | solution.py:47
  166.2 9.4 %fusion = f32[2,72,5184]{2,1,0:T(8,128)} fusion(f32[2,5184,72]{2,1,0:T(8,128)} %reshape.284, f32[72,5184]{1,0:T(8,128)S(1)} %fusion.5, s32[72]{0:T(128)S(1)} %add_select_fusion.1, pred[72]{0:T(512)(128)(4,1)S(1)} %iota_compare_fusion), kind=kOutput, calls=%fused_computation.3 | convolution fusion | flops 645770880 | bytes 7465320 | tf_op jit(solution)/shard_map/pmc,kc->pkm/dot_general | solution.py:47
  181.5 9.7 %convolution_bitcast_fusion.12 = f32[2,72,5184]{2,1,0:T(8,128)} fusion(f32[2,5184,72]{2,1,0:T(8,128)} %reshape.285, s32[72]{0:T(128)S(1)} %add_select_fusion.1, pred[72]{0:T(512)(128)(4,1)S(1)} %iota_compare_fusion), kind=kOutput, calls=%fused_computation.18 | convolution fusion | flops 645024384 | bytes 5972328 | tf_op jit(solution)/shard_map/pmk,kr->prm/dot_general | solution.py:51
  197.4 9.7 %convolution_bitcast_fusion.11 = f32[2,72,5184]{2,1,0:T(8,128)} fusion(f32[2,5184,72]{2,1,0:T(8,128)} %reshape.286, s32[72]{0:T(128)S(1)} %add_select_fusion.1, pred[72]{0:T(512)(128)(4,1)S(1)} %iota_compare_fusion), kind=kOutput, calls=%fused_computation.17 | convolution fusion | flops 645024384 | bytes 5972328 | tf_op jit(solution)/shard_map/pmk,kr->prm/dot_general | solution.py:51
  213.0 9.7 %convolution_bitcast_fusion.10 = f32[2,72,5184]{2,1,0:T(8,128)} fusion(f32[2,5184,72]{2,1,0:T(8,128)} %reshape.287, s32[72]{0:T(128)S(1)} %add_select_fusion.1, pred[72]{0:T(512)(128)(4,1)S(1)} %iota_compare_fusion), kind=kOutput, calls=%fused_computation.16 | convolution fusion | flops 645024384 | bytes 5972328 | tf_op jit(solution)/shard_map/pmk,kr->prm/dot_general | solution.py:51
  243.8 9.3 %convolution_bitcast_fusion.8 = f32[2,72,5184]{2,1,0:T(8,128)} fusion(f32[2,5184,72]{2,1,0:T(8,128)} %reshape.288, s32[72]{0:T(128)S(1)} %add_select_fusion.1, pred[72]{0:T(512)(128)(4,1)S(1)} %iota_compare_fusion), kind=kOutput, calls=%fused_computation.14 | convolution fusion | flops 645024384 | bytes 5972328 | tf_op jit(solution)/shard_map/pmc,kc->pkm/dot_general | solution.py:47
  274.3 9.6 %convolution_bitcast_fusion.7 = f32[2,72,5184]{2,1,0:T(8,128)} fusion(f32[2,5184,72]{2,1,0:T(8,128)} %reshape.290, s32[72]{0:T(128)S(1)} %add_select_fusion.1, pred[72]{0:T(512)(128)(4,1)S(1)} %iota_compare_fusion), kind=kOutput, calls=%fused_computation.13 | convolution fusion | flops 645024384 | bytes 5972328 | tf_op jit(solution)/shard_map/pmk,kr->prm/dot_general | solution.py:51
  290.1 9.6 %convolution_bitcast_fusion.6 = f32[2,72,5184]{2,1,0:T(8,128)} fusion(f32[2,5184,72]{2,1,0:T(8,128)} %reshape.291, s32[72]{0:T(128)S(1)} %add_select_fusion.1, pred[72]{0:T(512)(128)(4,1)S(1)} %iota_compare_fusion), kind=kOutput, calls=%fused_computation.12 | convolution fusion | flops 645024384 | bytes 5972328 | tf_op jit(solution)/shard_map/pmk,kr->prm/dot_general | solution.py:51
  305.5 9.6 %convolution_bitcast_fusion.5 = f32[2,72,5184]{2,1,0:T(8,128)} fusion(f32[2,5184,72]{2,1,0:T(8,128)} %reshape.292, s32[72]{0:T(128)S(1)} %add_select_fusion.1, pred[72]{0:T(512)(128)(4,1)S(1)} %iota_compare_fusion), kind=kOutput, calls=%fused_computation.11 | convolution fusion | flops 645024384 | bytes 5972328 | tf_op jit(solution)/shard_map/pmk,kr->prm/dot_general | solution.py:51
  321.1 9.4 %convolution_bitcast_fusion.4 = f32[2,72,5184]{2,1,0:T(8,128)} fusion(f32[2,5184,72]{2,1,0:T(8,128)} %reshape_reshape.11, s32[72]{0:T(128)S(1)} %add_select_fusion.1, pred[72]{0:T(512)(128)(4,1)S(1)} %iota_compare_fusion), kind=kOutput, calls=%fused_computation.10 | convolution fusion | flops 645024384 | bytes 5972328 | tf_op jit(solution)/shard_map/pmc,kc->pkm/dot_general | solution.py:47
  336.3 9.4 %convolution_bitcast_fusion.3 = f32[2,72,5184]{2,1,0:T(8,128)} fusion(f32[2,5184,72]{2,1,0:T(8,128)} %reshape.293, s32[72]{0:T(128)S(1)} %add_select_fusion.1, pred[72]{0:T(512)(128)(4,1)S(1)} %iota_compare_fusion), kind=kOutput, calls=%fused_computation.9 | convolution fusion | flops 645024384 | bytes 5972328 | tf_op jit(solution)/shard_map/pmc,kc->pkm/dot_general | solution.py:47
  351.8 9.4 %fusion.2 = f32[2,72,5184]{2,1,0:T(8,128)} fusion(f32[2,5184,72]{2,1,0:T(8,128)} %reshape.294, f32[72,5184]{1,0:T(8,128)S(1)} %fusion.5, s32[72]{0:T(128)S(1)} %add_select_fusion.1, pred[72]{0:T(512)(128)(4,1)S(1)} %iota_compare_fusion), kind=kOutput, calls=%fused_computation.5 | convolution fusion | flops 645770880 | bytes 7465320 | tf_op jit(solution)/shard_map/pmc,kc->pkm/dot_general | solution.py:47
  379.6 9.7 %convolution_bitcast_fusion.1 = f32[2,72,5184]{2,1,0:T(8,128)} fusion(f32[2,5184,72]{2,1,0:T(8,128)} %reshape.296, s32[72]{0:T(128)S(1)} %add_select_fusion.1, pred[72]{0:T(512)(128)(4,1)S(1)} %iota_compare_fusion), kind=kOutput, calls=%fused_computation.7 | convolution fusion | flops 645024384 | bytes 5972328 | tf_op jit(solution)/shard_map/pmk,kr->prm/dot_general | solution.py:51
  395.5 13.0 %multiply_reduce_fusion = (f32[72,5184]{1,0:T(8,128)S(1)}, f32[72,5184]{1,0:T(8,128)S(1)}, f32[72,5184]{1,0:T(8,128)S(1)}, f32[2,72,5184]{2,1,0:T(8,128)S(1)}) fusion(f32[2,72,5184]{2,0,1:T(2,128)S(1)} %copy-done.1, f32[2,72,5184]{2,1,0:T(8,128)} %convolution_bitcast_fusion.10, f32[2,72,5184]{2,1,0:T(8,128)} %convolution_bitcast_fusion.5, ...), kind=kOutput, calls=%fused_computation.21 | convolution fusion | flops 654355584 | bytes 23888232 | tf_op jit(solution)/shard_map/pmk,kr->prm/dot_general | solution.py:51
  408.7 20.7 %collective-permute-done.3 = f32[1,72,5184]{2,1,0:T(8,128)S(1)} collective-permute-done((f32[1,72,5184]{2,1,0:T(8,128)S(1)}, f32[1,72,5184]{2,1,0:T(8,128)S(1)}, u32[]{:S(2)}, u32[]{:S(2)}) %collective-permute-start.3) | collective-permute-done | bytes 1493024 | tf_op jit(solution)/shard_map/ppermute | solution.py:15
  430.2 20.0 %collective-permute-done.4 = f32[1,72,5184]{2,1,0:T(8,128)S(1)} collective-permute-done((f32[1,72,5184]{2,1,0:T(8,128)S(1)}, f32[1,72,5184]{2,1,0:T(8,128)S(1)}, u32[]{:S(2)}, u32[]{:S(2)}) %collective-permute-start.4) | collective-permute-done | bytes 1493024 | tf_op jit(solution)/shard_map/ppermute | solution.py:15
  450.4 18.3 %collective-permute-start.5 = (f32[1,72,5184]{2,1,0:T(8,128)S(1)}, f32[1,72,5184]{2,1,0:T(8,128)S(1)}, u32[]{:S(2)}, u32[]{:S(2)}) collective-permute-start(f32[1,72,5184]{2,1,0:T(8,128)S(1)} %bitcast_add_fusion), channel_id=1, source_target_pairs={{0,122},{2,124},{4,126},{6,0},{8,2},{10,4},{12,6},{14,8},{16,10},{... | collective-permute-start | bytes 4478984 | tf_op jit(solution)/shard_map/ppermute | solution.py:15
  468.7 22.2 %collective-permute-done.5 = f32[1,72,5184]{2,1,0:T(8,128)S(1)} collective-permute-done((f32[1,72,5184]{2,1,0:T(8,128)S(1)}, f32[1,72,5184]{2,1,0:T(8,128)S(1)}, u32[]{:S(2)}, u32[]{:S(2)}) %collective-permute-start.5) | collective-permute-done | bytes 1493024 | tf_op jit(solution)/shard_map/ppermute | solution.py:15
  492.8 36.3 %all_to_all.5 = f32[2,2,36,5184]{3,1,2,0:T(2,128)S(1)} all-to-all(f32[2,2,36,5184]{3,1,2,0:T(2,128)S(1)} %bitcast.126), channel_id=1, replica_groups=mesh['band'=64,'grid'=2] {'grid'}, dimensions={0} | all-to-all | bytes 5971968 | tf_op jit(solution)/shard_map/all_to_all | solution.py:25
  (68 shorter events, 160.6 us)
Async XLA Ops:
  6.5 50.6 %all-gather.2.cloned.1.call-start = ((), (), s32[]{:S(2)}) async-start(), calls=%async_computation.1 | async-start | bytes 4534272 | tf_op jit(solution)/shard_map/all_gather | solution.py:82
  60.2 20.8 %collective-permute-start = (f32[1,72,5184]{2,0,1:T(1,128)S(1)}, f32[1,72,5184]{2,0,1:T(1,128)S(1)}, u32[]{:S(2)}, u32[]{:S(2)}) collective-permute-start(f32[1,72,5184]{2,0,1:T(1,128)S(1)} %constant_dynamic-slice_fusion), channel_id=1, source_target_pairs={{0,2},{2,4},{4,6},{6,8},{8,10},{10,12},{12,14},{14,16},{16,18},{18... | collective-permute-start | bytes 4478984 | tf_op jit(solution)/shard_map/ppermute | solution.py:15
  81.0 1.1 copy-start.5
  82.1 20.8 %collective-permute-start.1 = (f32[1,72,5184]{2,0,1:T(1,128)S(1)}, f32[1,72,5184]{2,0,1:T(1,128)}, u32[]{:S(2)}, u32[]{:S(2)}) collective-permute-start(f32[1,72,5184]{2,0,1:T(1,128)S(1)} %collective-permute-done), channel_id=1, source_target_pairs={{0,2},{2,4},{4,6},{6,8},{8,10},{10,12},{12,14},{14,16},{16,18},{18... | collective-permute-start | bytes 4478984 | tf_op jit(solution)/shard_map/ppermute | solution.py:15
  102.9 21.0 %collective-permute-start.2 = (f32[1,72,5184]{2,0,1:T(1,128)}, f32[1,72,5184]{2,0,1:T(1,128)}, u32[]{:S(2)}, u32[]{:S(2)}) collective-permute-start(f32[1,72,5184]{2,0,1:T(1,128)} %collective-permute-done.1), channel_id=1, source_target_pairs={{0,2},{2,4},{4,6},{6,8},{8,10},{10,12},{12,14},{14,16},{16,18},{18... | collective-permute-start | bytes 4478984 | tf_op jit(solution)/shard_map/ppermute | solution.py:15
  108.6 2.5 copy-start.6
  111.2 14.3 %copy-start.2 = (f32[1,72,5184]{2,1,0:T(8,128)}, f32[1,72,5184]{2,1,0:T(8,128)S(1)}, u32[]{:S(2)}) copy-start(f32[1,72,5184]{2,1,0:T(8,128)S(1)} %copy.143) | copy-start | bytes 4478980
  111.2 14.3 %copy-start = (f32[2,72,5184]{2,0,1:T(2,128)S(1)}, f32[2,72,5184]{2,0,1:T(2,128)}, u32[]{:S(2)}) copy-start(f32[2,72,5184]{2,0,1:T(2,128)} %all-gather.2.cloned.1.call-done) | copy-start | bytes 8957956
  113.3 16.3 %copy-start.3 = (f32[1,72,5184]{2,1,0:T(8,128)}, f32[1,72,5184]{2,1,0:T(8,128)S(1)}, u32[]{:S(2)}) copy-start(f32[1,72,5184]{2,1,0:T(8,128)S(1)} %copy.142) | copy-start | bytes 4478980
  125.4 4.1 copy-start.4
  389.3 6.1 %copy-start.1 = (f32[2,72,5184]{2,0,1:T(2,128)S(1)}, f32[2,72,5184]{2,0,1:T(2,128)}, u32[]{:S(2)}) copy-start(f32[2,72,5184]{2,0,1:T(2,128)} %all-gather.2.cloned.1.call-done) | copy-start | bytes 8957956
  408.6 20.8 %collective-permute-start.3 = (f32[1,72,5184]{2,1,0:T(8,128)S(1)}, f32[1,72,5184]{2,1,0:T(8,128)S(1)}, u32[]{:S(2)}, u32[]{:S(2)}) collective-permute-start(f32[1,72,5184]{2,1,0:T(8,128)S(1)} %negate_bitcast_fusion), channel_id=1, source_target_pairs={{0,2},{2,4},{4,6},{6,8},{8,10},{10,12},{12,14},{14,16},{16,18},{18... | collective-permute-start | bytes 4478984 | tf_op jit(solution)/shard_map/ppermute | solution.py:15
  429.5 20.8 %collective-permute-start.4 = (f32[1,72,5184]{2,1,0:T(8,128)S(1)}, f32[1,72,5184]{2,1,0:T(8,128)S(1)}, u32[]{:S(2)}, u32[]{:S(2)}) collective-permute-start(f32[1,72,5184]{2,1,0:T(8,128)S(1)} %bitcast_add_fusion.1), channel_id=1, source_target_pairs={{0,2},{2,4},{4,6},{6,8},{8,10},{10,12},{12,14},{14,16},{16,18},{18... | collective-permute-start | bytes 4478984 | tf_op jit(solution)/shard_map/ppermute | solution.py:15
  450.4 40.5 %collective-permute-start.5 = (f32[1,72,5184]{2,1,0:T(8,128)S(1)}, f32[1,72,5184]{2,1,0:T(8,128)S(1)}, u32[]{:S(2)}, u32[]{:S(2)}) collective-permute-start(f32[1,72,5184]{2,1,0:T(8,128)S(1)} %bitcast_add_fusion), channel_id=1, source_target_pairs={{0,122},{2,124},{4,126},{6,0},{8,2},{10,4},{12,6},{14,8},{16,10},{... | collective-permute-start | bytes 4478984 | tf_op jit(solution)/shard_map/ppermute | solution.py:15
Sparse Core Ops, SparseCore 0:
  9.0 48.0 all-gather.1
where the time goes:
time: 548 us; the launch traced here: 540 us
  matrix products  173 us (32%)
  waiting for transfers between devices  165 us (30%)
  local copies, waits for them, and re-layouts  121 us (22%)
  blocking collectives  36.3 us (7%)
  starting transfers between devices  19.2 us (4%)
  between operations  13.8 us (3%)
  other arithmetic  11.4 us (2%)
    ppermute x6, waiting for transfers between devices, shifted(): return lax.ppermute(value, axis, pairs)  115 us
    dot_general x9, matrix products, inverse_axis(): jnp.einsum('pmk,kr->prm', values, table, precision=lax.Precision.HIGHEST)  88.6 us
    dot_general x9, matrix products, forward_axis(): jnp.einsum('pmc,kc->pkm', values, table, precision=lax.Precision.HIGHEST)  84.5 us
    reshape x9, local copies, waits for them, and re-layouts, coulomb_filter(): work = inverse_axis(work.reshape(pairs, count * count, count), table)  52.3 us
    all_gather x1, waiting for transfers between devices, local(): whole = lax.all_gather(bands, 'grid', axis=1, tiled=True)  49.8 us
    all_to_all x1, blocking collectives, sent_and_summed(): lax.all_to_all(split_up(array, dim, devices), axis, 0, 0, tiled=True)  36.3 us
    reshape x6, local copies, waits for them, and re-layouts, coulomb_filter(): work = forward_axis(work.reshape(pairs, count * count, count), table)  35.6 us
    ppermute x6, starting transfers between devices, shifted(): return lax.ppermute(value, axis, pairs)  19.2 us
  transfers between devices with their start and end apart: 7, of which 7 were waited for; matrix products, arithmetic and copies ran while one was open for 2% of the time, Pallas kernels for 0%

commit v1 on v0

--- a/solution.py
+++ b/solution.py
@@ -79,7 +79,9 @@
 
 def local(bands):
     table, kernel = tables(GRID)
-    whole = lax.all_gather(bands, "grid", axis=1, tiled=True)
+    whole = jnp.concatenate(
+        lax.all_to_all(jnp.stack([bands] * lax.axis_size("grid")), "grid", 0, 0), axis=1
+    )
     share = whole.shape[0] // lax.axis_size("grid")
     first = lax.axis_index("grid") * share
     visit = lax.dynamic_slice_in_dim(whole, first, share, 0)

time: 548 us -> 504 us (0.920)
  waiting for transfers between devices: 165 us -> 107 us
  other arithmetic: 11.4 us -> 32.9 us
  between operations: 13.8 us -> 0.42 us
  local copies, waits for them, and re-layouts: 121 us -> 130 us
    all_gather x1 -> x0, waiting for transfers between devices: 49.8 us -> none  [local(): whole = lax.all_gather(bands, 'grid', axis=1, tiled=True)]
    ppermute x6, waiting for transfers between devices: 115 us -> 71.8 us  [shifted(): return lax.ppermute(value, axis, pairs)]
    all_to_all x0 -> x1, waiting for transfers between devices: none -> 34.8 us  [local(): lax.all_to_all(jnp.stack([bands] * lax.axis_size('grid')), 'grid', 0, 0)]
    ppermute x0 -> x3, other arithmetic: none -> 18.4 us  [shifted(): return lax.ppermute(value, axis, pairs)]
    another operation x3 -> x1, local copies, waits for them, and re-layouts: 18 us -> 5.92 us  [pair_terms(): home[:, None] * visit[None]]
    mul x0 -> x3, local copies, waits for them, and re-layouts: none -> 11.3 us  [pair_terms(): home[:, None] * visit[None]]
    ppermute x6, starting transfers between devices: 19.2 us -> 12.8 us  [shifted(): return lax.ppermute(value, axis, pairs)]
  transfers between devices with their start and end apart: 7 -> 7, of which waited for: 7 -> 4; matrix products, arithmetic and copies ran while one was open for 2% -> 28% of each run, Pallas kernels for 0% -> 0%
where the time goes in v1:
time: 504 us; the launch traced here: 499 us
  matrix products  178 us (35%)
  local copies, waits for them, and re-layouts  130 us (26%)
  waiting for transfers between devices  107 us (21%)
  blocking collectives  34.3 us (7%)
  other arithmetic  32.9 us (7%)
  starting transfers between devices  16.7 us (3%)
    dot_general x9, matrix products, inverse_axis(): jnp.einsum('pmk,kr->prm', values, table, precision=lax.Precision.HIGHEST)  89.2 us
    dot_general x9, matrix products, forward_axis(): jnp.einsum('pmc,kc->pkm', values, table, precision=lax.Precision.HIGHEST)  88.7 us
    ppermute x6, waiting for transfers between devices, shifted(): return lax.ppermute(value, axis, pairs)  71.8 us
    reshape x9, local copies, waits for them, and re-layouts, coulomb_filter(): work = inverse_axis(work.reshape(pairs, count * count, count), table)  53.4 us
    reshape x6, local copies, waits for them, and re-layouts, coulomb_filter(): work = forward_axis(work.reshape(pairs, count * count, count), table)  35.2 us
    all_to_all x1, waiting for transfers between devices, local(): lax.all_to_all(jnp.stack([bands] * lax.axis_size('grid')), 'grid', 0, 0)  34.8 us
    all_to_all x1, blocking collectives, sent_and_summed(): lax.all_to_all(split_up(array, dim, devices), axis, 0, 0, tiled=True)  34.3 us
    ppermute x3, other arithmetic, shifted(): return lax.ppermute(value, axis, pairs)  18.4 us
  transfers between devices with their start and end apart: 7, of which 4 were waited for; matrix products, arithmetic and copies ran while one was open for 28% of the time, Pallas kernels for 0%

profile of v1, /device:TPU:4, one launch (start us, length us, event | category | flops | bytes accessed | tf_op | source)
XLA Modules:
  0.0 498.5 jit_solution(2676811077681852908)
XLA Ops:
  9.0 34.8 %all-to-all-done = f32[2,2,36,5184]{3,1,2,0:T(2,128)S(1)} async-done(((f32[2,2,36,5184]{3,1,2,0:T(2,128)}), f32[2,2,36,5184]{3,1,2,0:T(2,128)S(1)}, u32[]{:S(2)}, u32[]{:S(2)}) %all-to-all-start) | async-done | bytes 2986016 | tf_op jit(solution)/shard_map/all_to_all | solution.py:83
  78.2 10.4 %convolution_bitcast_fusion.14 = f32[2,72,5184]{2,1,0:T(8,128)} fusion(f32[2,5184,72]{2,1,0:T(8,128)} %broadcast_in_dim_reshape.2, f32[5184,72]{1,0:T(8,128)} %mul.373, s32[72]{0:T(128)S(1)} %add_select_fusion.1, pred[72]{0:T(512)(128)(4,1)S(1)} %iota_compare_fusion), kind=kOutput, calls=%fused_computation.20 | convolution fusion | flops 645770880 | bytes 7465320 | tf_op jit(solution)/shard_map/pmc,kc->pkm/dot_general | solution.py:47
  94.5 9.4 %convolution_bitcast_fusion.13 = f32[2,72,5184]{2,1,0:T(8,128)} fusion(f32[2,5184,72]{2,1,0:T(8,128)} %reshape.306, s32[72]{0:T(128)S(1)} %add_select_fusion.1, pred[72]{0:T(512)(128)(4,1)S(1)} %iota_compare_fusion), kind=kOutput, calls=%fused_computation.19 | convolution fusion | flops 645024384 | bytes 5972328 | tf_op jit(solution)/shard_map/pmc,kc->pkm/dot_general | solution.py:47
  111.9 9.9 %fusion = f32[2,72,5184]{2,1,0:T(8,128)} fusion(f32[2,5184,72]{2,1,0:T(8,128)} %reshape.307, f32[72,5184]{1,0:T(8,128)} %fusion.11, s32[72]{0:T(128)S(1)} %add_select_fusion.1, pred[72]{0:T(512)(128)(4,1)S(1)} %iota_compare_fusion), kind=kOutput, calls=%fused_computation.3 | convolution fusion | flops 645770880 | bytes 7465320 | tf_op jit(solution)/shard_map/pmc,kc->pkm/dot_general | solution.py:47
  127.7 9.7 %convolution_bitcast_fusion.12 = f32[2,72,5184]{2,1,0:T(8,128)} fusion(f32[2,5184,72]{2,1,0:T(8,128)} %reshape.308, s32[72]{0:T(128)S(1)} %add_select_fusion.1, pred[72]{0:T(512)(128)(4,1)S(1)} %iota_compare_fusion), kind=kOutput, calls=%fused_computation.18 | convolution fusion | flops 645024384 | bytes 5972328 | tf_op jit(solution)/shard_map/pmk,kr->prm/dot_general | solution.py:51
  143.3 9.7 %convolution_bitcast_fusion.11 = f32[2,72,5184]{2,1,0:T(8,128)} fusion(f32[2,5184,72]{2,1,0:T(8,128)} %reshape.309, s32[72]{0:T(128)S(1)} %add_select_fusion.1, pred[72]{0:T(512)(128)(4,1)S(1)} %iota_compare_fusion), kind=kOutput, calls=%fused_computation.17 | convolution fusion | flops 645024384 | bytes 5972328 | tf_op jit(solution)/shard_map/pmk,kr->prm/dot_general | solution.py:51
  161.8 9.7 %convolution_bitcast_fusion.10 = f32[2,72,5184]{2,1,0:T(8,128)} fusion(f32[2,5184,72]{2,1,0:T(8,128)} %reshape.310, s32[72]{0:T(128)S(1)} %add_select_fusion.1, pred[72]{0:T(512)(128)(4,1)S(1)} %iota_compare_fusion), kind=kOutput, calls=%fused_computation.16 | convolution fusion | flops 645024384 | bytes 5972328 | tf_op jit(solution)/shard_map/pmk,kr->prm/dot_general | solution.py:51
  181.3 10.3 %convolution_bitcast_fusion.9 = f32[2,72,5184]{2,1,0:T(8,128)} fusion(f32[2,5184,72]{2,1,0:T(8,128)} %broadcast_in_dim_reshape.2, f32[5184,72]{1,0:T(8,128)} %mul.393, s32[72]{0:T(128)S(1)} %add_select_fusion.1, pred[72]{0:T(512)(128)(4,1)S(1)} %iota_compare_fusion), kind=kOutput, calls=%fused_computation.15 | convolution fusion | flops 645770880 | bytes 7465320 | tf_op jit(solution)/shard_map/pmc,kc->pkm/dot_general | solution.py:47
  197.5 9.3 %convolution_bitcast_fusion.8 = f32[2,72,5184]{2,1,0:T(8,128)} fusion(f32[2,5184,72]{2,1,0:T(8,128)} %reshape.311, s32[72]{0:T(128)S(1)} %add_select_fusion.1, pred[72]{0:T(512)(128)(4,1)S(1)} %iota_compare_fusion), kind=kOutput, calls=%fused_computation.14 | convolution fusion | flops 645024384 | bytes 5972328 | tf_op jit(solution)/shard_map/pmc,kc->pkm/dot_general | solution.py:47
  213.2 9.8 %fusion.1 = f32[2,72,5184]{2,1,0:T(8,128)} fusion(f32[2,5184,72]{2,1,0:T(8,128)} %reshape.312, f32[72,5184]{1,0:T(8,128)} %fusion.11, s32[72]{0:T(128)S(1)} %add_select_fusion.1, pred[72]{0:T(512)(128)(4,1)S(1)} %iota_compare_fusion), kind=kOutput, calls=%fused_computation.4 | convolution fusion | flops 645770880 | bytes 7465320 | tf_op jit(solution)/shard_map/pmc,kc->pkm/dot_general | solution.py:47
  228.8 9.6 %convolution_bitcast_fusion.7 = f32[2,72,5184]{2,1,0:T(8,128)} fusion(f32[2,5184,72]{2,1,0:T(8,128)} %reshape.313, s32[72]{0:T(128)S(1)} %add_select_fusion.1, pred[72]{0:T(512)(128)(4,1)S(1)} %iota_compare_fusion), kind=kOutput, calls=%fused_computation.13 | convolution fusion | flops 645024384 | bytes 5972328 | tf_op jit(solution)/shard_map/pmk,kr->prm/dot_general | solution.py:51
  244.3 9.6 %convolution_bitcast_fusion.6 = f32[2,72,5184]{2,1,0:T(8,128)} fusion(f32[2,5184,72]{2,1,0:T(8,128)} %reshape.314, s32[72]{0:T(128)S(1)} %add_select_fusion.1, pred[72]{0:T(512)(128)(4,1)S(1)} %iota_compare_fusion), kind=kOutput, calls=%fused_computation.12 | convolution fusion | flops 645024384 | bytes 5972328 | tf_op jit(solution)/shard_map/pmk,kr->prm/dot_general | solution.py:51
  262.5 9.6 %convolution_bitcast_fusion.5 = f32[2,72,5184]{2,1,0:T(8,128)} fusion(f32[2,5184,72]{2,1,0:T(8,128)} %reshape.315, s32[72]{0:T(128)S(1)} %add_select_fusion.1, pred[72]{0:T(512)(128)(4,1)S(1)} %iota_compare_fusion), kind=kOutput, calls=%fused_computation.11 | convolution fusion | flops 645024384 | bytes 5972328 | tf_op jit(solution)/shard_map/pmk,kr->prm/dot_general | solution.py:51
  282.2 10.3 %convolution_bitcast_fusion.4 = f32[2,72,5184]{2,1,0:T(8,128)} fusion(f32[2,5184,72]{2,1,0:T(8,128)} %broadcast_in_dim_reshape.2, f32[5184,72]{1,0:T(8,128)} %mul.401, s32[72]{0:T(128)S(1)} %add_select_fusion.1, pred[72]{0:T(512)(128)(4,1)S(1)} %iota_compare_fusion), kind=kOutput, calls=%fused_computation.10 | convolution fusion | flops 645770880 | bytes 7465320 | tf_op jit(solution)/shard_map/pmc,kc->pkm/dot_general | solution.py:47
  298.3 9.3 %convolution_bitcast_fusion.3 = f32[2,72,5184]{2,1,0:T(8,128)} fusion(f32[2,5184,72]{2,1,0:T(8,128)} %reshape.316, s32[72]{0:T(128)S(1)} %add_select_fusion.1, pred[72]{0:T(512)(128)(4,1)S(1)} %iota_compare_fusion), kind=kOutput, calls=%fused_computation.9 | convolution fusion | flops 645024384 | bytes 5972328 | tf_op jit(solution)/shard_map/pmc,kc->pkm/dot_general | solution.py:47
  313.7 9.8 %fusion.2 = f32[2,72,5184]{2,1,0:T(8,128)} fusion(f32[2,5184,72]{2,1,0:T(8,128)} %reshape.317, f32[72,5184]{1,0:T(8,128)} %fusion.11, s32[72]{0:T(128)S(1)} %add_select_fusion.1, pred[72]{0:T(512)(128)(4,1)S(1)} %iota_compare_fusion), kind=kOutput, calls=%fused_computation.5 | convolution fusion | flops 645770880 | bytes 7465320 | tf_op jit(solution)/shard_map/pmc,kc->pkm/dot_general | solution.py:47
  329.3 9.6 %convolution_bitcast_fusion.2 = f32[2,72,5184]{2,1,0:T(8,128)} fusion(f32[2,5184,72]{2,1,0:T(8,128)} %reshape.318, s32[72]{0:T(128)S(1)} %add_select_fusion.1, pred[72]{0:T(512)(128)(4,1)S(1)} %iota_compare_fusion), kind=kOutput, calls=%fused_computation.8 | convolution fusion | flops 645024384 | bytes 5972328 | tf_op jit(solution)/shard_map/pmk,kr->prm/dot_general | solution.py:51
  344.7 9.6 %convolution_bitcast_fusion.1 = f32[2,72,5184]{2,1,0:T(8,128)} fusion(f32[2,5184,72]{2,1,0:T(8,128)} %reshape.319, s32[72]{0:T(128)S(1)} %add_select_fusion.1, pred[72]{0:T(512)(128)(4,1)S(1)} %iota_compare_fusion), kind=kOutput, calls=%fused_computation.7 | convolution fusion | flops 645024384 | bytes 5972328 | tf_op jit(solution)/shard_map/pmk,kr->prm/dot_general | solution.py:51
  362.7 12.0 %multiply_reduce_fusion = (f32[72,5184]{1,0:T(8,128)S(1)}, f32[72,5184]{1,0:T(8,128)S(1)}, f32[72,5184]{1,0:T(8,128)S(1)}, f32[2,72,5184]{2,1,0:T(8,128)S(1)}) fusion(f32[2,72,5184]{2,0,1:T(2,128)S(1)} %bitcast.123, f32[2,72,5184]{2,1,0:T(8,128)} %convolution_bitcast_fusion.5, f32[2,72,5184]{2,1,0:T(8,128)S(1)} %copy-done, f32[72,5184]{1,0:T(8,128)S(1)} %bitcast.127, ...), kind=kOutput, calls=%fused_computation.25 | convolution fusion | flops 654355584 | bytes 23888232 | tf_op jit(solution)/shard_map/pmk,kr->prm/dot_general | solution.py:51
  377.9 17.7 %collective-permute-done.3 = f32[1,72,5184]{2,1,0:T(8,128)S(1)} collective-permute-done((f32[1,72,5184]{2,1,0:T(8,128)S(1)}, f32[1,72,5184]{2,1,0:T(8,128)S(1)}, u32[]{:S(2)}, u32[]{:S(2)}) %collective-permute-start.3) | collective-permute-done | bytes 1493024 | tf_op jit(solution)/shard_map/ppermute | solution.py:15
  395.8 20.7 %collective-permute-done.4 = f32[1,72,5184]{2,1,0:T(8,128)S(1)} collective-permute-done((f32[1,72,5184]{2,1,0:T(8,128)S(1)}, f32[1,72,5184]{2,1,0:T(8,128)S(1)}, u32[]{:S(2)}, u32[]{:S(2)}) %collective-permute-start.4) | collective-permute-done | bytes 1493024 | tf_op jit(solution)/shard_map/ppermute | solution.py:15
  416.7 6.7 %collective-permute-start.5 = (f32[1,72,5184]{2,1,0:T(8,128)S(1)}, f32[1,72,5184]{2,1,0:T(8,128)S(1)}, u32[]{:S(2)}, u32[]{:S(2)}) collective-permute-start(f32[1,72,5184]{2,1,0:T(8,128)S(1)} %bitcast_add_fusion), channel_id=1, source_target_pairs={{0,122},{2,124},{4,126},{6,0},{8,2},{10,4},{12,6},{14,8},{16,10},{... | collective-permute-start | bytes 4478984 | tf_op jit(solution)/shard_map/ppermute | solution.py:15
  423.4 33.5 %collective-permute-done.5 = f32[1,72,5184]{2,1,0:T(8,128)S(1)} collective-permute-done((f32[1,72,5184]{2,1,0:T(8,128)S(1)}, f32[1,72,5184]{2,1,0:T(8,128)S(1)}, u32[]{:S(2)}, u32[]{:S(2)}) %collective-permute-start.5) | collective-permute-done | bytes 1493024 | tf_op jit(solution)/shard_map/ppermute | solution.py:15
  458.8 34.3 %all_to_all.10 = f32[2,2,36,5184]{3,1,2,0:T(2,128)} all-to-all(f32[2,2,36,5184]{3,1,2,0:T(2,128)S(1)} %bitcast.124), channel_id=1, replica_groups=mesh['band'=64,'grid'=2] {'grid'}, dimensions={0} | all-to-all | bytes 5971968 | tf_op jit(solution)/shard_map/all_to_all | solution.py:25
  (60 shorter events, 172.6 us)
Async XLA Ops:
  4.9 38.9 %all-to-all-start = ((f32[2,2,36,5184]{3,1,2,0:T(2,128)}), f32[2,2,36,5184]{3,1,2,0:T(2,128)S(1)}, u32[]{:S(2)}, u32[]{:S(2)}) async-start(f32[2,2,36,5184]{3,1,2,0:T(2,128)} %pad_maximum_fusion), calls=%async_computation | async-start | bytes 6045696 | tf_op jit(solution)/shard_map/all_to_all | solution.py:83
  46.3 22.0 %collective-permute-start = (f32[1,72,5184]{2,0,1:T(1,128)}, f32[1,72,5184]{2,0,1:T(1,128)}, u32[]{:S(2)}, u32[]{:S(2)}) collective-permute-start(f32[1,72,5184]{2,0,1:T(1,128)} %constant_dynamic-slice_fusion), channel_id=1, source_target_pairs={{0,2},{2,4},{4,6},{6,8},{8,10},{10,12},{12,14},{14,16},{16,18},{18... | collective-permute-start | bytes 4478984 | tf_op jit(solution)/shard_map/ppermute | solution.py:15
  109.8 61.8 %collective-permute-start.1 = (f32[1,72,5184]{2,0,1:T(1,128)}, f32[1,72,5184]{2,0,1:T(1,128)}, u32[]{:S(2)}, u32[]{:S(2)}) collective-permute-start(f32[1,72,5184]{2,0,1:T(1,128)} %collective-permute-done), channel_id=1, source_target_pairs={{0,2},{2,4},{4,6},{6,8},{8,10},{10,12},{12,14},{14,16},{16,18},{18... | collective-permute-start | bytes 4478984 | tf_op jit(solution)/shard_map/ppermute | solution.py:15
  212.7 59.5 %collective-permute-start.2 = (f32[1,72,5184]{2,0,1:T(1,128)}, f32[1,72,5184]{2,0,1:T(1,128)}, u32[]{:S(2)}, u32[]{:S(2)}) collective-permute-start(f32[1,72,5184]{2,0,1:T(1,128)} %collective-permute-done.1), channel_id=1, source_target_pairs={{0,2},{2,4},{4,6},{6,8},{8,10},{10,12},{12,14},{14,16},{16,18},{18... | collective-permute-start | bytes 4478984 | tf_op jit(solution)/shard_map/ppermute | solution.py:15
  360.4 2.3 copy-start
  374.8 20.8 %collective-permute-start.3 = (f32[1,72,5184]{2,1,0:T(8,128)S(1)}, f32[1,72,5184]{2,1,0:T(8,128)S(1)}, u32[]{:S(2)}, u32[]{:S(2)}) collective-permute-start(f32[1,72,5184]{2,1,0:T(8,128)S(1)} %negate_bitcast_fusion), channel_id=1, source_target_pairs={{0,2},{2,4},{4,6},{6,8},{8,10},{10,12},{12,14},{14,16},{16,18},{18... | collective-permute-start | bytes 4478984 | tf_op jit(solution)/shard_map/ppermute | solution.py:15
  395.7 20.8 %collective-permute-start.4 = (f32[1,72,5184]{2,1,0:T(8,128)S(1)}, f32[1,72,5184]{2,1,0:T(8,128)S(1)}, u32[]{:S(2)}, u32[]{:S(2)}) collective-permute-start(f32[1,72,5184]{2,1,0:T(8,128)S(1)} %bitcast_add_fusion.1), channel_id=1, source_target_pairs={{0,2},{2,4},{4,6},{6,8},{8,10},{10,12},{12,14},{14,16},{16,18},{18... | collective-permute-start | bytes 4478984 | tf_op jit(solution)/shard_map/ppermute | solution.py:15
  416.7 40.2 %collective-permute-start.5 = (f32[1,72,5184]{2,1,0:T(8,128)S(1)}, f32[1,72,5184]{2,1,0:T(8,128)S(1)}, u32[]{:S(2)}, u32[]{:S(2)}) collective-permute-start(f32[1,72,5184]{2,1,0:T(8,128)S(1)} %bitcast_add_fusion), channel_id=1, source_target_pairs={{0,122},{2,124},{4,126},{6,0},{8,2},{10,4},{12,6},{14,8},{16,10},{... | collective-permute-start | bytes 4478984 | tf_op jit(solution)/shard_map/ppermute | solution.py:15
